TPU v7x, 32 devices: a whole 2x2x4 slice. The times are simulated.
32 devices in a mesh: expert: 4 (over y, core), shard: 8 (over z, x).
Axes of the slice: x: 2, y: 2, z: 4, core: 2. Of those that a mesh axis runs over, the one named last changes fastest.
Arguments:
- master_down: float32 [16, 6400, 4096], P('expert', None, 'shard'), may hold values from -0.109375 to 0.109375
- second_down: bfloat16 [16, 6400, 4096], P('expert', None, 'shard'), may hold values from -0.0390625 to 0.0390625
- router_weight: float32 [4096, 16], P('shard', 'expert'), may hold values from -0.09375 to 0.09375
- router_gain: float32 [4096], P('shard'), may hold values from 0.25 to 1.75
Outputs:
- final_down: bfloat16 [16, 6400, 4096], P('expert', 'shard')
- scale_down: float32 [16, 6400], P('expert', 'shard')
- serve_router: bfloat16 [4096, 16], replicated
All inputs are finite; a program needn't handle non-finite values.
Results may differ from a plain program's by a relative error of at most 0.0085.
Values may be sent and summed in bfloat16 or wider, within the bound.
A program may use at most 256 MiB of HBM per device.

v0:
```python
import jax
import jax.numpy as jnp
from jax import lax
from jax.sharding import PartitionSpec as P


def body(master_down, second_down, router_weight, router_gain):
    merged_down = master_down + second_down.astype(jnp.float32)
    total_down = lax.psum(
        jnp.sum(merged_down * merged_down, axis=2).astype(jnp.bfloat16), "shard"
    ).astype(jnp.float32)
    scale_down = jnp.sqrt(total_down)
    narrow_down = (merged_down / jnp.expand_dims(scale_down, 2)).astype(jnp.bfloat16)
    final_down = lax.all_to_all(narrow_down, "shard", split_axis=1, concat_axis=2, tiled=True)
    scale_down = lax.dynamic_slice_in_dim(
        scale_down, lax.axis_index("shard") * final_down.shape[1], final_down.shape[1], axis=1
    )
    part_router = (router_weight * router_gain[:, None]).astype(jnp.bfloat16)
    row_router = lax.all_gather(part_router, "shard", axis=0, tiled=True)
    serve_router = lax.all_gather(row_router, "expert", axis=1, tiled=True)
    return (final_down, scale_down, serve_router)


def solution(mesh):
    placed = (
        P("expert", None, "shard"),
        P("expert", None, "shard"),
        P("shard", "expert"),
        P("shard"),
    )
    return jax.shard_map(
        body,
        mesh=mesh,
        in_specs=placed,
        out_specs=(P("expert", "shard", None), P("expert", "shard"), P()),
        check_vma=False,
    )
```

profile of v0, /device:TPU:0, one launch (start us, length us, event | category | flops | bytes accessed | tf_op | source)
XLA Modules:
  0.0 826.9 jit_solution(7862156734528137198)
XLA Ops:
  0.6 24.2 %multiply_reduce_fusion = bf16[4,6400]{1,0:T(4,128)(2,1)S(1)} fusion(f32[4,6400,512]{2,1,0:T(8,128)} %param.4, bf16[4,6400,512]{2,1,0:T(8,128)(2,1)} %param.5), kind=kLoop, calls=%fused_computation.1 | loop fusion | flops 52403200 | bytes 78694400 | tf_op jit(solution)/shard_map/reduce_sum | solution.py:10
  24.9 0.9 copy.21
  25.8 83.5 %psum.7 = bf16[4,6400]{0,1:T(8,128)(2,1)} all-reduce(bf16[4,6400]{0,1:T(8,128)(2,1)S(1)} %copy.21), channel_id=1, replica_groups=mesh['expert'=4,'shard'=8] {'shard'}, use_global_device_ids=true, to_apply=%region_1.0 | all-reduce | flops 25600 | bytes 102400 | tf_op jit(solution)/shard_map/psum | solution.py:9
  109.3 2.3 convert_sqrt_fusion
  111.6 1.2 copy.17
  112.8 34.3 %divide_convert_fusion = bf16[4,6400,512]{2,1,0:T(8,128)(2,1)} fusion(f32[4,6400,512]{2,1,0:T(8,128)} %param.4, bf16[4,6400,512]{2,1,0:T(8,128)(2,1)} %param.5, f32[4,6400]{1,0:T(4,128)S(1)} %copy.17), kind=kLoop, calls=%fused_computation | loop fusion | flops 52428800 | bytes 104960000 | tf_op jit(solution)/shard_map/convert_element_type | solution.py:13
  147.1 33.4 %copy.18 = bf16[4,6400,512]{2,0,1:T(4,128)(2,1)} copy(bf16[4,6400,512]{2,1,0:T(8,128)(2,1)} %divide_convert_fusion) | data formatting | bytes 52428800 | tf_op jit(solution)/shard_map/convert_element_type | solution.py:13
  180.5 0.0 copy-start
  180.5 0.0 copy-start.1
  180.5 6.6 all-to-all-start
  187.2 0.8 constant_dynamic-slice_fusion
  187.9 1.8 copy.20
  189.7 0.0 copy-done
  189.7 0.0 copy-done.1
  189.7 573.7 %all_gather.6 = bf16[4096,4]{0,1:T(4,128)(2,1)S(1)} all-gather(bf16[512,4]{0,1:T(4,128)(2,1)S(1)} %multiply_convert_fusion), channel_id=1, replica_groups=mesh['expert'=4,'shard'=8] {'shard'}, dimensions={0}, use_global_device_ids=true | all-gather | bytes 36864 | tf_op jit(solution)/shard_map/all_gather | solution.py:19
  763.4 5.4 all-gather
  768.8 0.7 reshape.9
  769.5 0.0 all-to-all-done
  769.5 18.2 %copy.19 = bf16[4,800,8,512]{3,2,1,0:T(8,128)(2,1)} copy(bf16[4,800,8,512]{3,0,1,2:T(4,128)(2,1)} %bitcast.1) | data formatting | bytes 52428800 | tf_op jit(solution)/shard_map/all_to_all | solution.py:14
  787.7 39.2 %all_to_all.16 = bf16[4,800,4096]{2,1,0:T(8,128)(2,1)} reshape(bf16[4,800,8,512]{3,2,1,0:T(8,128)(2,1)} %copy.19) | data formatting | bytes 52428800 | tf_op jit(solution)/shard_map/all_to_all | solution.py:14
  (1 shorter events, 0.0 us)
Async XLA Ops:
  180.5 9.2 %copy-start = (f32[512,4]{0,1:T(4,128)S(1)}, f32[512,4]{0,1:T(4,128)}, u32[]{:S(2)}) copy-start(f32[512,4]{0,1:T(4,128)} %param.6) | copy-start | bytes 24580
  180.5 9.2 %copy-start.1 = (f32[512]{0:T(512)S(1)}, f32[512]{0:T(512)}, u32[]{:S(2)}) copy-start(f32[512]{0:T(512)} %param.7) | copy-start | bytes 6148
  180.5 589.0 %all-to-all-start = ((bf16[4,6400,512]{2,0,1:T(4,128)(2,1)}), bf16[4,6400,512]{2,0,1:T(4,128)(2,1)}, u32[]{:S(2)}, u32[]{:S(2)}) async-start(bf16[4,6400,512]{2,0,1:T(4,128)(2,1)} %copy.18), calls=%async_computation | async-start | bytes 52428800 | tf_op jit(solution)/shard_map/all_to_all | solution.py:14
where the time goes:
time: 828 us; the launch traced here: 827 us
  blocking collectives  663 us (80%)
  local copies, waits for them, and re-layouts  96.2 us (12%)
  other arithmetic  60.8 us (7%)
    all_gather x1, blocking collectives, body(): row_router = lax.all_gather(part_router, 'shard', axis=0, tiled=True)  574 us
    psum x1, blocking collectives, body(): lax.psum(jnp.sum(merged_down * merged_down, axis=2).astype(jnp.bfloat16),...  83.5 us
    all_to_all x2, local copies, waits for them, and re-layouts, body(): lax.all_to_all(narrow_down, 'shard', split_axis=1, concat_axis=2, tiled=T...  57.4 us
    convert_element_type x1, other arithmetic, body(): (merged_down / jnp.expand_dims(scale_down, 2)).astype(jnp.bfloat16)  34.3 us
    convert_element_type x1, local copies, waits for them, and re-layouts, body(): (merged_down / jnp.expand_dims(scale_down, 2)).astype(jnp.bfloat16)  33.4 us
    reduce_sum x1, other arithmetic, body(): jnp.sum(merged_down * merged_down, axis=2).astype(jnp.bfloat16)  24.2 us
  transfers between devices with their start and end apart: 1, of which 0 were waited for; matrix products, arithmetic and copies ran while one was open for 0% of the time, Pallas kernels for 0%

commit v1 on v0

--- a/solution.py
+++ b/solution.py
@@ -4,9 +4,14 @@
 from jax.sharding import PartitionSpec as P
 
 
+def add_all(x, axis):
+    parts = lax.all_gather(x, axis)
+    return jnp.sum(parts, axis=0)
+
+
 def body(master_down, second_down, router_weight, router_gain):
     merged_down = master_down + second_down.astype(jnp.float32)
-    total_down = lax.psum(
+    total_down = add_all(
         jnp.sum(merged_down * merged_down, axis=2).astype(jnp.bfloat16), "shard"
     ).astype(jnp.float32)
     scale_down = jnp.sqrt(total_down)

time: 828 us -> 779 us (0.941)
  blocking collectives: 663 us -> 618 us
    psum x1 -> x0, blocking collectives: 83.5 us -> none  [body(): lax.psum(jnp.sum(merged_down * merged_down, axis=2).astype(jnp.bfloat16),...]
    all_gather x0 -> x1, blocking collectives: none -> 32.8 us  [add_all(): parts = lax.all_gather(x, axis)]
where the time goes in v1:
time: 779 us; the launch traced here: 777 us
  blocking collectives  618 us (79%)
  local copies, waits for them, and re-layouts  93.8 us (12%)
  other arithmetic  58.8 us (8%)
    all_gather x1, blocking collectives, body(): row_router = lax.all_gather(part_router, 'shard', axis=0, tiled=True)  579 us
    all_to_all x2, local copies, waits for them, and re-layouts, body(): lax.all_to_all(narrow_down, 'shard', split_axis=1, concat_axis=2, tiled=T...  57.4 us
    convert_element_type x1, other arithmetic, body(): (merged_down / jnp.expand_dims(scale_down, 2)).astype(jnp.bfloat16)  34.3 us
    convert_element_type x1, local copies, waits for them, and re-layouts, body(): (merged_down / jnp.expand_dims(scale_down, 2)).astype(jnp.bfloat16)  33.4 us
    all_gather x1, blocking collectives, add_all(): parts = lax.all_gather(x, axis)  32.8 us
    reduce_sum x1, other arithmetic, body(): jnp.sum(merged_down * merged_down, axis=2).astype(jnp.bfloat16)  24.2 us
  transfers between devices with their start and end apart: 1, of which 0 were waited for; matrix products, arithmetic and copies ran while one was open for 0% of the time, Pallas kernels for 0%

profile of v1, /device:TPU:0, one launch (start us, length us, event | category | flops | bytes accessed | tf_op | source)
XLA Modules:
  0.0 777.5 jit_solution(17265991484088323087)
XLA Ops:
  0.6 24.2 %multiply_reduce_fusion = bf16[4,6400]{1,0:T(4,128)(2,1)S(1)} fusion(f32[4,6400,512]{2,1,0:T(8,128)} %param.4, bf16[4,6400,512]{2,1,0:T(8,128)(2,1)} %param.5), kind=kLoop, calls=%fused_computation.1 | loop fusion | flops 52403200 | bytes 78694400 | tf_op jit(solution)/shard_map/reduce_sum | solution.py:15
  24.9 0.9 copy.21
  25.8 0.8 copy.18
  26.6 32.8 %all-gather.1 = bf16[8,4,6400]{2,1,0:T(4,128)(2,1)S(1)} all-gather(bf16[1,4,6400]{2,1,0:T(4,128)(2,1)S(1)} %copy.18), channel_id=2, replica_groups=mesh['expert'=4,'shard'=8] {'shard'}, dimensions={0}, use_global_device_ids=true | all-gather | bytes 460800 | tf_op jit(solution)/shard_map/all_gather | solution.py:8
  59.4 0.2 reduce_sum.22
  59.6 0.1 convert_sqrt_fusion
  59.6 34.3 %divide_convert_fusion = bf16[4,6400,512]{2,1,0:T(8,128)(2,1)} fusion(f32[4,6400,512]{2,1,0:T(8,128)} %param.4, bf16[4,6400,512]{2,1,0:T(8,128)(2,1)} %param.5, f32[4,6400]{1,0:T(4,128)S(1)} %convert_sqrt_fusion), kind=kLoop, calls=%fused_computation | loop fusion | flops 52428800 | bytes 104960000 | tf_op jit(solution)/shard_map/convert_element_type | solution.py:18
  93.9 0.0 copy-start
  93.9 0.0 copy-start.1
  93.9 33.4 %copy.19 = bf16[4,6400,512]{2,0,1:T(4,128)(2,1)} copy(bf16[4,6400,512]{2,1,0:T(8,128)(2,1)} %divide_convert_fusion) | data formatting | bytes 52428800 | tf_op jit(solution)/shard_map/convert_element_type | solution.py:18
  127.3 6.5 all-to-all-start
  133.8 0.0 copy-done
  133.8 0.0 copy-done.1
  133.9 579.4 %all_gather.11 = bf16[4096,4]{0,1:T(4,128)(2,1)S(1)} all-gather(bf16[512,4]{0,1:T(4,128)(2,1)S(1)} %multiply_convert_fusion), channel_id=1, replica_groups=mesh['expert'=4,'shard'=8] {'shard'}, dimensions={0}, use_global_device_ids=true | all-gather | bytes 36864 | tf_op jit(solution)/shard_map/all_gather | solution.py:24
  713.3 5.4 all-gather.2
  718.7 0.7 reshape.23
  719.4 0.7 constant_dynamic-slice_fusion
  720.1 0.0 all-to-all-done
  720.1 18.2 %copy.20 = bf16[4,800,8,512]{3,2,1,0:T(8,128)(2,1)} copy(bf16[4,800,8,512]{3,0,1,2:T(4,128)(2,1)} %bitcast.2) | data formatting | bytes 52428800 | tf_op jit(solution)/shard_map/all_to_all | solution.py:19
  738.3 39.2 %all_to_all.16 = bf16[4,800,4096]{2,1,0:T(8,128)(2,1)} reshape(bf16[4,800,8,512]{3,2,1,0:T(8,128)(2,1)} %copy.20) | data formatting | bytes 52428800 | tf_op jit(solution)/shard_map/all_to_all | solution.py:19
  (1 shorter events, 0.0 us)
Async XLA Ops:
  93.9 39.9 %copy-start = (f32[512,4]{0,1:T(4,128)S(1)}, f32[512,4]{0,1:T(4,128)}, u32[]{:S(2)}) copy-start(f32[512,4]{0,1:T(4,128)} %param.6) | copy-start | bytes 24580
  93.9 39.9 %copy-start.1 = (f32[512]{0:T(512)S(1)}, f32[512]{0:T(512)}, u32[]{:S(2)}) copy-start(f32[512]{0:T(512)} %param.7) | copy-start | bytes 6148
  127.3 592.7 %all-to-all-start = ((bf16[4,6400,512]{2,0,1:T(4,128)(2,1)}), bf16[4,6400,512]{2,0,1:T(4,128)(2,1)}, u32[]{:S(2)}, u32[]{:S(2)}) async-start(bf16[4,6400,512]{2,0,1:T(4,128)(2,1)} %copy.19), calls=%async_computation | async-start | bytes 52428800 | tf_op jit(solution)/shard_map/all_to_all | solution.py:19

commit v2 on v0

--- a/solution.py
+++ b/solution.py
@@ -11,7 +11,10 @@
     ).astype(jnp.float32)
     scale_down = jnp.sqrt(total_down)
     narrow_down = (merged_down / jnp.expand_dims(scale_down, 2)).astype(jnp.bfloat16)
-    final_down = lax.all_to_all(narrow_down, "shard", split_axis=1, concat_axis=2, tiled=True)
+    n_dev = lax.axis_size("shard")
+    shards = jnp.stack(jnp.split(narrow_down, n_dev, axis=1), axis=0)
+    shards = lax.all_to_all(shards, "shard", split_axis=0, concat_axis=0)
+    final_down = jnp.concatenate(shards, axis=2)
     scale_down = lax.dynamic_slice_in_dim(
         scale_down, lax.axis_index("shard") * final_down.shape[1], final_down.shape[1], axis=1
     )

time: 828 us -> 739 us (0.89)
  local copies, waits for them, and re-layouts: 96.2 us -> 49.8 us
  blocking collectives: 663 us -> 623 us
    all_to_all x2 -> x0, local copies, waits for them, and re-layouts: 57.4 us -> none  [body(): lax.all_to_all(narrow_down, 'shard', split_axis=1, concat_axis=2, tiled=T...]
    psum x1, blocking collectives: 83.5 us -> 39.3 us  [body(): lax.psum(jnp.sum(merged_down * merged_down, axis=2).astype(jnp.bfloat16),...]
    convert_element_type x1 -> x0, local copies, waits for them, and re-layouts: 33.4 us -> none  [body(): (merged_down / jnp.expand_dims(scale_down, 2)).astype(jnp.bfloat16)]
    unnamed x7 -> x12, local copies, waits for them, and re-layouts: 3.4 us -> 27.5 us
    reshape x0 -> x1, local copies, waits for them, and re-layouts: none -> 17.9 us  [body(): final_down = jnp.concatenate(shards, axis=2)]
where the time goes in v2:
time: 739 us
  blocking collectives  623 us (84%)
  other arithmetic  58.6 us (8%)
  local copies, waits for them, and re-layouts  49.8 us (7%)
    all_gather x1, blocking collectives, body(): row_router = lax.all_gather(part_router, 'shard', axis=0, tiled=True)  578 us
    psum x1, blocking collectives, body(): lax.psum(jnp.sum(merged_down * merged_down, axis=2).astype(jnp.bfloat16),...  39.3 us
    convert_element_type x1, other arithmetic, body(): (merged_down / jnp.expand_dims(scale_down, 2)).astype(jnp.bfloat16)  34.3 us
    unnamed x12, local copies, waits for them, and re-layouts  27.5 us
    reduce_sum x1, other arithmetic, body(): jnp.sum(merged_down * merged_down, axis=2).astype(jnp.bfloat16)  24.2 us
    reshape x1, local copies, waits for them, and re-layouts, body(): final_down = jnp.concatenate(shards, axis=2)  17.9 us
  transfers between devices with their start and end apart: 1, of which 0 were waited for; matrix products, arithmetic and copies ran while one was open for 0% of the time, Pallas kernels for 0%

profile of v2, /device:TPU:0, one launch (start us, length us, event | category | flops | bytes accessed | tf_op | source)
XLA Modules:
  0.0 738.6 jit_solution(8709787585122454427)
XLA Ops:
  0.6 24.2 %multiply_reduce_fusion = bf16[4,6400]{1,0:T(4,128)(2,1)S(1)} fusion(f32[4,6400,512]{2,1,0:T(8,128)} %param.4, bf16[4,6400,512]{2,1,0:T(8,128)(2,1)} %param.5), kind=kLoop, calls=%fused_computation.1 | loop fusion | flops 52403200 | bytes 78694400 | tf_op jit(solution)/shard_map/reduce_sum | solution.py:10
  24.9 39.3 %psum.7 = bf16[4,6400]{1,0:T(4,128)(2,1)S(1)} all-reduce(bf16[4,6400]{1,0:T(4,128)(2,1)S(1)} %multiply_reduce_fusion), channel_id=1, replica_groups=mesh['expert'=4,'shard'=8] {'shard'}, use_global_device_ids=true, to_apply=%region_1.0 | all-reduce | flops 25600 | bytes 102400 | tf_op jit(solution)/shard_map/psum | solution.py:9
  64.2 0.1 convert_sqrt_fusion
  64.3 34.3 %divide_convert_fusion = bf16[4,6400,512]{2,1,0:T(8,128)(2,1)} fusion(f32[4,6400,512]{2,1,0:T(8,128)} %param.4, bf16[4,6400,512]{2,1,0:T(8,128)(2,1)} %param.5, f32[4,6400]{1,0:T(4,128)S(1)} %convert_sqrt_fusion), kind=kLoop, calls=%fused_computation | loop fusion | flops 52428800 | bytes 104960000 | tf_op jit(solution)/shard_map/convert_element_type | solution.py:13
  98.5 3.8 fusion.7
  102.4 3.8 fusion.6
  106.2 3.8 fusion.5
  110.0 3.8 fusion.4
  113.8 3.9 fusion.3
  117.7 3.8 fusion.2
  121.5 3.8 fusion.1
  125.3 3.8 fusion
  129.1 0.0 copy-start
  129.1 0.0 copy-start.1
  129.1 6.6 all-to-all-start
  135.8 0.0 copy-done
  135.8 0.0 copy-done.1
  135.8 578.1 %all_gather.6 = bf16[4096,4]{0,1:T(4,128)(2,1)S(1)} all-gather(bf16[512,4]{0,1:T(4,128)(2,1)S(1)} %multiply_convert_fusion), channel_id=1, replica_groups=mesh['expert'=4,'shard'=8] {'shard'}, dimensions={0}, use_global_device_ids=true | all-gather | bytes 36864 | tf_op jit(solution)/shard_map/all_gather | solution.py:22
  714.0 5.4 all-gather
  719.4 0.7 reshape.17
  720.1 0.7 constant_dynamic-slice_fusion
  720.7 0.0 all-to-all-done
  720.7 17.9 %copy.9 = bf16[8,4,100,8,512]{4,3,0,2,1:T(8,128)(2,1)} copy(bf16[8,4,100,8,512]{4,3,2,1,0:T(8,128)(2,1)} %bitcast.13) | data formatting | bytes 52428800 | tf_op jit(solution)/shard_map/reshape | solution.py:17
  (1 shorter events, 0.0 us)
Async XLA Ops:
  129.1 6.6 copy-start
  129.1 6.7 copy-start.1
  129.1 591.6 %all-to-all-start = ((bf16[8,4,800,512]{3,2,1,0:T(8,128)(2,1)}), bf16[8,4,800,512]{3,2,1,0:T(8,128)(2,1)}, u32[]{:S(2)}, u32[]{:S(2)}) async-start(bf16[8,4,800,512]{3,2,1,0:T(8,128)(2,1)} %fusion), calls=%async_computation | async-start | bytes 52428800 | tf_op jit(solution)/shard_map/all_to_all | solution.py:16
